TPU v7x, 32 devices: a whole 2x2x4 slice. The times are simulated.
32 devices in a mesh: dp: 4 (over x, core), seq: 2 (over y), tensor: 4 (over z).
Axes of the slice: x: 2, y: 2, z: 4, core: 2. Of those that a mesh axis runs over, the one named last changes fastest.
Arguments:
- tokens: bfloat16 [2048, 4096], P(('dp', 'seq')), may hold values from -6 to 6
- seg_ids: int32 [2048], P('dp'), may hold values from 0 to 15, as said below
- gain_attn: bfloat16 [4096], P(('dp', 'seq')), may hold values from 0.5 to 1.5
- w_query: bfloat16 [4096, 4096], P(('dp', 'seq'), 'tensor'), may hold values from -1.5 to 1.5
- kv_weight: bfloat16 [4096, 512], P(('dp', 'seq')), may hold values from -1.5 to 1.5
- w_out: bfloat16 [4096, 4096], P('tensor', ('dp', 'seq')), may hold values from -0.375 to 0.375
- gain_ffn: bfloat16 [4096], P(('dp', 'seq')), may hold values from 0.5 to 1.5
- w_gate: bfloat16 [4096, 12288], P(('dp', 'seq'), 'tensor'), may hold values from -0.09375 to 0.09375
- w_up: bfloat16 [4096, 12288], P(('dp', 'seq'), 'tensor'), may hold values from -0.09375 to 0.09375
- w_down: bfloat16 [12288, 4096], P('tensor', ('dp', 'seq')), may hold values from -0.0546875 to 0.0546875
- d_out: bfloat16 [2048, 4096], P(('dp', 'seq')), may hold values from -6 to 6
Outputs:
- out: bfloat16 [2048, 4096], P(('dp', 'seq'))
- d_tokens: float32 [2048, 4096], P(('dp', 'seq'))
- d_gain_attn: float32 [4096], P(('dp', 'seq'))
- d_w_query: float32 [4096, 4096], P(('dp', 'seq'), 'tensor')
- d_kv_weight: float32 [4096, 512], P(('dp', 'seq'))
- d_w_out: float32 [4096, 4096], P('tensor', ('dp', 'seq'))
- d_gain_ffn: float32 [4096], P(('dp', 'seq'))
- d_w_gate: float32 [4096, 12288], P(('dp', 'seq'), 'tensor')
- d_w_up: float32 [4096, 12288], P(('dp', 'seq'), 'tensor')
- d_w_down: float32 [12288, 4096], P('tensor', ('dp', 'seq'))
Inputs may be any that keep to these rules, and one draw needn't show every extreme that they name: `seg_ids`: within each group of 512 tokens g (from 0) the ids never fall, take values from 4 g to 4 g + 3 and start at 4 g; some group other than the last holds one sequence.
All inputs are finite; a program needn't handle non-finite values.
Results may differ from a plain program's by a relative error of at most 0.02.
Values may be sent and summed in bfloat16 or wider, within the bound.
A program may use at most 384 MiB of HBM per device.

v0:
```python
import math
import jax
import jax.numpy as jnp
from jax import lax
from jax.sharding import PartitionSpec as P

HD = 256
EPS = 1e-06
NEG = -1e30


def place_tables(segs):
    length = segs.shape[0]
    index = jnp.arange(length, dtype=jnp.int32)
    flags = jnp.concatenate([jnp.ones((1,), dtype=bool), segs[1:] != segs[:-1]])
    starts = lax.cummax(jnp.where(flags, index, jnp.zeros_like(index)), axis=0)
    places = index - starts
    half_size = HD // 2
    freqs = jnp.exp(jnp.arange(half_size, dtype=jnp.float32) * (-math.log(10000.0) / half_size))
    angles = places.astype(jnp.float32)[:, None] * freqs[None, :]
    return (places, jnp.cos(angles), jnp.sin(angles))


def rotate(vector, cos_table, sin_table):
    half_size = vector.shape[-1] // 2
    leading = vector[..., :half_size]
    trailing = vector[..., half_size:]
    return jnp.concatenate(
        [leading * cos_table - trailing * sin_table, trailing * cos_table + leading * sin_table],
        axis=-1,
    )


def rotate_back(vector, cos_table, sin_table):
    half_size = vector.shape[-1] // 2
    leading = vector[..., :half_size]
    trailing = vector[..., half_size:]
    return jnp.concatenate(
        [leading * cos_table + trailing * sin_table, trailing * cos_table - leading * sin_table],
        axis=-1,
    )


def matmul(left, right):
    return jnp.dot(left, right, preferred_element_type=jnp.float32)


def matmul_nt(left, right):
    return lax.dot_general(
        left, right, (((1,), (1,)), ((), ())), preferred_element_type=jnp.float32
    )


def matmul_tn(left, right):
    return lax.dot_general(
        left, right, (((0,), (0,)), ((), ())), preferred_element_type=jnp.float32
    )


def gelu_tanh(values):
    return jax.nn.gelu(values, approximate=True)


def norm_back(d_act, normed, rms_val, gain_val):
    scaled = d_act * gain_val
    return rms_val * (scaled - normed * jnp.mean(scaled * normed, axis=-1, keepdims=True))


def shards(
    tokens, seg_ids, gain_attn, w_query, kv_weight, w_out, gain_ffn, w_gate, w_up, w_down, d_out
):
    rows = tokens.shape[0]
    scale_factor = 1.0 / math.sqrt(HD)
    offset = lax.axis_index("seq") * rows
    places, cos_table, sin_table = place_tables(seg_ids)
    own_places = lax.dynamic_slice_in_dim(places, offset, rows, 0)
    own_segs = lax.dynamic_slice_in_dim(seg_ids, offset, rows, 0)
    own_cos = lax.dynamic_slice_in_dim(cos_table, offset, rows, 0)
    own_sin = lax.dynamic_slice_in_dim(sin_table, offset, rows, 0)
    allowed = (own_segs[:, None] == seg_ids[None, :]) & (own_places[:, None] >= places[None, :])
    full_query, full_out, full_kv, full_gain_one = (
        lax.all_gather(w_query, ("dp", "seq"), axis=0, tiled=True),
        lax.all_gather(w_out, ("dp", "seq"), axis=1, tiled=True),
        lax.all_gather(kv_weight, ("dp", "seq"), axis=0, tiled=True),
        lax.all_gather(gain_attn, ("dp", "seq"), axis=0, tiled=True),
    )
    gain_one = full_gain_one.astype(jnp.float32)
    inputs = tokens.astype(jnp.float32)
    rms_one = lax.rsqrt(jnp.mean(inputs * inputs, axis=-1, keepdims=True) + EPS)
    norm_one = inputs * rms_one
    act_one = (norm_one * gain_one).astype(jnp.bfloat16)
    query_pre = matmul(act_one, full_query)
    heads = query_pre.shape[1] // HD
    kv_pre = matmul(act_one, full_kv)
    queries = (
        rotate(query_pre.reshape(rows, heads, HD), own_cos[:, None, :], own_sin[:, None, :])
        * scale_factor
    ).astype(jnp.bfloat16)
    own_kv = jnp.concatenate(
        [rotate(kv_pre[:, :HD], own_cos, own_sin), kv_pre[:, HD:]], axis=1
    ).astype(jnp.bfloat16)
    all_kv = lax.all_gather(own_kv, "seq", axis=0, tiled=True)
    keys = all_kv[:, :HD]
    values_all = all_kv[:, HD:]
    scores = jnp.einsum("rhd,kd->hrk", queries, keys, preferred_element_type=jnp.float32)
    scores = jnp.where(allowed[None], scores, NEG)
    top_score = jnp.max(scores, axis=-1, keepdims=True)
    expd = jnp.exp(scores - top_score)
    total = jnp.sum(expd, axis=-1, keepdims=True)
    log_total = top_score + jnp.log(total)
    probs_low = (expd / total).astype(jnp.bfloat16)
    mixed = (
        jnp.einsum("hrk,kd->rhd", probs_low, values_all, preferred_element_type=jnp.float32)
        .reshape(rows, heads * HD)
        .astype(jnp.bfloat16)
    )
    attn = lax.psum(matmul(mixed, full_out), "tensor")
    resid = inputs + attn
    full_gate, full_up, full_down, full_gain_two = (
        lax.all_gather(w_gate, ("dp", "seq"), axis=0, tiled=True),
        lax.all_gather(w_up, ("dp", "seq"), axis=0, tiled=True),
        lax.all_gather(w_down, ("dp", "seq"), axis=1, tiled=True),
        lax.all_gather(gain_ffn, ("dp", "seq"), axis=0, tiled=True),
    )
    gain_two = full_gain_two.astype(jnp.float32)
    rms_two = lax.rsqrt(jnp.mean(resid * resid, axis=-1, keepdims=True) + EPS)
    norm_two = resid * rms_two
    act_two = (norm_two * gain_two).astype(jnp.bfloat16)
    gate = matmul(act_two, full_gate)
    up_val = matmul(act_two, full_up)
    gelu_val, gelu_pull = jax.vjp(gelu_tanh, gate)
    hidden = (gelu_val * up_val).astype(jnp.bfloat16)
    ffn = lax.psum(matmul(hidden, full_down).astype(jnp.bfloat16), "tensor").astype(jnp.float32)
    out = (resid + ffn).astype(jnp.bfloat16)
    back_gate, back_up, back_down = (
        lax.all_gather(w_gate, ("dp", "seq"), axis=0, tiled=True),
        lax.all_gather(w_up, ("dp", "seq"), axis=0, tiled=True),
        lax.all_gather(w_down, ("dp", "seq"), axis=1, tiled=True),
    )
    d_hidden = matmul_nt(d_out, back_down)
    grad_down = matmul_tn(hidden, d_out)
    d_gate = gelu_pull(d_hidden * up_val)[0].astype(jnp.bfloat16)
    d_up = (d_hidden * gelu_val).astype(jnp.bfloat16)
    grad_gate = matmul_tn(act_two, d_gate)
    grad_up = matmul_tn(act_two, d_up)
    d_act_two = lax.psum(matmul_nt(d_gate, back_gate) + matmul_nt(d_up, back_up), "tensor")
    grad_gain_two = jnp.sum(d_act_two * norm_two, axis=0)
    d_resid = d_out.astype(jnp.float32) + norm_back(d_act_two, norm_two, rms_two, gain_two)
    ffn_grads = (
        lax.psum_scatter(
            grad_gate.astype(jnp.bfloat16), ("dp", "seq"), scatter_dimension=0, tiled=True
        ).astype(jnp.float32),
        lax.psum_scatter(
            grad_up.astype(jnp.bfloat16), ("dp", "seq"), scatter_dimension=0, tiled=True
        ).astype(jnp.float32),
        lax.psum_scatter(
            grad_down.astype(jnp.bfloat16), ("dp", "seq"), scatter_dimension=1, tiled=True
        ).astype(jnp.float32),
        lax.psum_scatter(
            grad_gain_two.astype(jnp.bfloat16), ("dp", "seq"), scatter_dimension=0, tiled=True
        ).astype(jnp.float32),
    )
    back_query, back_out, back_kv = (
        lax.all_gather(w_query, ("dp", "seq"), axis=0, tiled=True),
        lax.all_gather(w_out, ("dp", "seq"), axis=1, tiled=True),
        lax.all_gather(kv_weight, ("dp", "seq"), axis=0, tiled=True),
    )
    d_attn = d_resid.astype(jnp.bfloat16)
    grad_out = matmul_tn(mixed, d_attn)
    d_mixed = matmul_nt(d_attn, back_out).astype(jnp.bfloat16).reshape(rows, heads, HD)
    scores_again = jnp.einsum("rhd,kd->hrk", queries, keys, preferred_element_type=jnp.float32)
    probs = jnp.where(allowed[None], jnp.exp(scores_again - log_total), 0.0)
    d_probs = jnp.einsum("rhd,kd->hrk", d_mixed, values_all, preferred_element_type=jnp.float32)
    delta = jnp.sum(probs * d_probs, axis=-1, keepdims=True)
    d_scores = (probs * (d_probs - delta)).astype(jnp.bfloat16)
    d_queries = (
        jnp.einsum("hrk,kd->rhd", d_scores, keys, preferred_element_type=jnp.float32) * scale_factor
    )
    d_query_pre = (
        rotate_back(d_queries, own_cos[:, None, :], own_sin[:, None, :])
        .reshape(rows, heads * HD)
        .astype(jnp.bfloat16)
    )
    d_keys_part = jnp.einsum("hrk,rhd->kd", d_scores, queries, preferred_element_type=jnp.float32)
    d_values_part = jnp.einsum(
        "hrk,rhd->kd", probs.astype(jnp.bfloat16), d_mixed, preferred_element_type=jnp.float32
    )
    own_kv_grad = lax.psum_scatter(
        jnp.concatenate([d_keys_part, d_values_part], axis=1).astype(jnp.bfloat16),
        "seq",
        scatter_dimension=0,
        tiled=True,
    )
    d_act_query = matmul_nt(d_query_pre, back_query)
    d_act_sum, kv_grad = (
        lax.psum(d_act_query.astype(jnp.bfloat16), "tensor").astype(jnp.float32),
        lax.psum(own_kv_grad, "tensor").astype(jnp.float32),
    )
    d_kv_pre = jnp.concatenate(
        [rotate_back(kv_grad[:, :HD], own_cos, own_sin), kv_grad[:, HD:]], axis=1
    ).astype(jnp.bfloat16)
    d_act_one = d_act_sum + matmul_nt(d_kv_pre, back_kv)
    grad_query = matmul_tn(act_one, d_query_pre)
    grad_kv = matmul_tn(act_one, d_kv_pre)
    grad_gain_one = jnp.sum(d_act_one * norm_one, axis=0)
    d_tokens = d_resid + norm_back(d_act_one, norm_one, rms_one, gain_one)
    attn_grads = (
        lax.psum_scatter(
            grad_query.astype(jnp.bfloat16), ("dp", "seq"), scatter_dimension=0, tiled=True
        ).astype(jnp.float32),
        lax.psum_scatter(
            grad_out.astype(jnp.bfloat16), ("dp", "seq"), scatter_dimension=1, tiled=True
        ).astype(jnp.float32),
        lax.psum_scatter(
            grad_kv.astype(jnp.bfloat16), ("dp", "seq"), scatter_dimension=0, tiled=True
        ).astype(jnp.float32),
        lax.psum_scatter(
            grad_gain_one.astype(jnp.bfloat16), ("dp", "seq"), scatter_dimension=0, tiled=True
        ).astype(jnp.float32),
    )
    return (
        out,
        d_tokens,
        attn_grads[3],
        attn_grads[0],
        attn_grads[2],
        attn_grads[1],
        ffn_grads[3],
        ffn_grads[0],
        ffn_grads[1],
        ffn_grads[2],
    )


def solution(mesh):
    in_specs = (
        P(("dp", "seq"), None),
        P("dp"),
        P(("dp", "seq")),
        P(("dp", "seq"), "tensor"),
        P(("dp", "seq"), None),
        P("tensor", ("dp", "seq")),
        P(("dp", "seq")),
        P(("dp", "seq"), "tensor"),
        P(("dp", "seq"), "tensor"),
        P("tensor", ("dp", "seq")),
        P(("dp", "seq"), None),
    )
    out_specs = (
        P(("dp", "seq"), None),
        P(("dp", "seq"), None),
        P(("dp", "seq")),
        P(("dp", "seq"), "tensor"),
        P(("dp", "seq"), None),
        P("tensor", ("dp", "seq")),
        P(("dp", "seq")),
        P(("dp", "seq"), "tensor"),
        P(("dp", "seq"), "tensor"),
        P("tensor", ("dp", "seq")),
    )
    return jax.shard_map(shards, mesh=mesh, in_specs=in_specs, out_specs=out_specs, check_vma=False)
```

profile of v0, /device:TPU:0, one launch (start us, length us, event | category | flops | bytes accessed | tf_op | source)
XLA Modules:
  0.0 1815.9 jit_solution(10553113912535316646)
XLA Ops:
  12.5 18.0 all-gather
  31.5 17.9 all-gather.9.cloned.1.call-done
  49.4 3.5 fusion.48
  53.7 10.2 all_gather.35
  63.8 42.2 %all-gather.11.cloned.1.call-done = bf16[4096,1024]{1,0:T(8,128)(2,1)} async-done(((bf16[512,1024]{1,0:T(8,128)(2,1)}), bf16[4096,1024]{1,0:T(8,128)(2,1)}) %all-gather.11.cloned.1.call-update) | async-done | bytes 8388624 | tf_op jit(solution)/shard_map/all_gather | solution.py:82
  106.1 6.8 fusion.46
  120.8 43.1 %all-gather.13.cloned.1.call-done = bf16[1024,4096]{1,0:T(8,128)(2,1)} async-done(((bf16[1024,512]{1,0:T(8,128)(2,1)}), bf16[1024,4096]{1,0:T(8,128)(2,1)}) %all-gather.13.cloned.1.call-update) | async-done | bytes 8388624 | tf_op jit(solution)/shard_map/all_gather | solution.py:83
  163.8 8.0 fusion.51
  173.8 16.6 all-gather.1
  190.5 136.5 %all-reduce.8.cloned.1.call-done = f32[256,4096]{1,0:T(8,128)} async-done(((f32[256,4096]{1,0:T(8,128)}), f32[256,4096]{1,0:T(8,128)}) %all-reduce.8.cloned.1.call-update) | async-done | bytes 4194320 | tf_op jit(solution)/shard_map/psum | solution.py:117
  327.0 2.8 multiply_reduce_fusion.2
  333.7 119.2 %all-gather.17.cloned.1.call-done = bf16[4096,3072]{1,0:T(8,128)(2,1)} async-done(((bf16[512,3072]{1,0:T(8,128)(2,1)}), bf16[4096,3072]{1,0:T(8,128)(2,1)}) %all-gather.17.cloned.1.call-update) | async-done | bytes 25165840 | tf_op jit(solution)/shard_map/all_gather | solution.py:121
  452.9 13.7 fusion.53
  466.6 113.3 %all-gather.15.cloned.1.call-done = bf16[4096,3072]{1,0:T(8,128)(2,1)} async-done(((bf16[512,3072]{1,0:T(8,128)(2,1)}), bf16[4096,3072]{1,0:T(8,128)(2,1)}) %all-gather.15.cloned.1.call-update) | async-done | bytes 25165840 | tf_op jit(solution)/shard_map/all_gather | solution.py:120
  579.8 13.6 fusion.52
  593.4 118.5 %all-gather.19.cloned.1.call-done = bf16[3072,4096]{1,0:T(8,128)(2,1)} async-done(((bf16[3072,512]{1,0:T(8,128)(2,1)}), bf16[3072,4096]{1,0:T(8,128)(2,1)}) %all-gather.19.cloned.1.call-update) | async-done | bytes 25165840 | tf_op jit(solution)/shard_map/all_gather | solution.py:122
  711.9 17.4 multiply_convert_fusion.1
  729.3 13.4 fusion.54
  742.7 14.7 convolution_add_fusion.1
  758.8 13.8 convolution_convert_fusion.7
  772.6 140.0 %all-reduce.10.cloned.1.call-done = f32[256,4096]{1,0:T(8,128)} async-done(((f32[256,4096]{1,0:T(8,128)}), f32[256,4096]{1,0:T(8,128)}) %all-reduce.10.cloned.1.call-update) | async-done | bytes 4194320 | tf_op jit(solution)/shard_map/psum | solution.py:146
  912.6 5.4 multiply_reduce_fusion
  918.5 3.1 multiply_add_fusion
  923.7 6.5 convolution_convert_fusion.8
  932.2 2.3 fusion.28
  939.2 7.1 convolution_convert_fusion.6
  946.3 5.3 reduce-scatter.8.cloned.1.call-done
  951.7 166.4 %all-reduce.12.cloned.1.call-done = (bf16[256,4096]{1,0:T(8,128)(2,1)}, bf16[256,4096]{1,0:T(8,128)(2,1)}, bf16[256,512]{1,0:T(8,128)(2,1)}) async-done(((bf16[256,4096]{1,0:T(8,128)(2,1)}, bf16[256,4096]{1,0:T(8,128)(2,1)}, bf16[256,512]{1,0:T(8,128)(2,1)}), (bf16[256,4096]{1,0:T(8,128)(2,1)}, bf16[256,4096]{1,0:T(8,128)(2,1)}, bf16[256,512]{1,0:T(8,128)(2,1)})) %all-reduce.12.cloned.1.call-update) | async-done | bytes 4456464 | tf_op jit(solution)/shard_map/psum | solution.py:133
  1120.8 3.5 convolution_convert_fusion.5
  1125.3 8.3 convolution_convert_fusion.3
  1133.7 5.8 convolution_convert_fusion.4
  1140.0 13.7 convolution_convert_fusion
  1153.7 13.9 convolution_convert_fusion.1
  1167.7 13.5 convolution_convert_fusion.2
  1183.1 7.2 fusion.9
  1190.3 25.7 %all-reduce.2 = (bf16[4096]{0:T(1024)(128)(2,1)S(1)}, bf16[4096]{0:T(1024)(128)(2,1)S(1)}) all-reduce(bf16[4096]{0:T(1024)(128)(2,1)S(1)} %get-tuple-element.12, bf16[4096]{0:T(1024)(128)(2,1)S(1)} %copy-done.22), channel_id=3, replica_groups=mesh['dp'=4,'seq'=2,'tensor'=4] {'dp','seq'}, use_global_device_ids=true, to_apply=%region_16.17.clone | all-reduce | flops 8192 | bytes 32768
  1216.6 10.6 fusion.8
  1227.2 2.1 convert_element_type.165
  1229.4 20.3 %reduce-scatter.14.cloned.1.call-done = bf16[1024,512]{1,0:T(8,128)(2,1)} async-done(((bf16[1024,4096]{1,0:T(8,128)(2,1)}), bf16[1024,512]{1,0:T(8,128)(2,1)}) %reduce-scatter.14.cloned.1.call-update) | async-done | bytes 1048592 | tf_op jit(solution)/shard_map/reduce_scatter | solution.py:211
  1249.7 2.8 convert_element_type.167
  1252.5 72.2 %reduce-scatter.10.cloned.1.call-done = bf16[512,1024]{1,0:T(8,128)(2,1)} async-done(((bf16[4096,1024]{1,0:T(8,128)(2,1)}), bf16[512,1024]{1,0:T(8,128)(2,1)}) %reduce-scatter.10.cloned.1.call-update) | async-done | bytes 1048592 | tf_op jit(solution)/shard_map/reduce_scatter | solution.py:208
  1324.7 2.8 convert_element_type.163
  1327.4 156.7 %reduce-scatter.20.cloned.1.call-done = bf16[3072,512]{1,0:T(8,128)(2,1)} async-done(((bf16[3072,4096]{1,0:T(8,128)(2,1)}), bf16[3072,512]{1,0:T(8,128)(2,1)}) %reduce-scatter.20.cloned.1.call-update) | async-done | bytes 3145744 | tf_op jit(solution)/shard_map/reduce_scatter | solution.py:156
  1484.2 5.5 convert_element_type.175
  1489.7 154.3 %reduce-scatter.18.cloned.1.call-done = bf16[512,3072]{1,0:T(8,128)(2,1)} async-done(((bf16[4096,3072]{1,0:T(8,128)(2,1)}), bf16[512,3072]{1,0:T(8,128)(2,1)}) %reduce-scatter.18.cloned.1.call-update) | async-done | bytes 3145744 | tf_op jit(solution)/shard_map/reduce_scatter | solution.py:153
  1644.0 5.4 convert_element_type.173
  1649.4 154.4 %reduce-scatter.16.cloned.1.call-done = bf16[512,3072]{1,0:T(8,128)(2,1)} async-done(((bf16[4096,3072]{1,0:T(8,128)(2,1)}), bf16[512,3072]{1,0:T(8,128)(2,1)}) %reduce-scatter.16.cloned.1.call-update) | async-done | bytes 3145744 | tf_op jit(solution)/shard_map/reduce_scatter | solution.py:150
  1803.8 5.4 convert_element_type.171
  (143 shorter events, 37.3 us)
Async XLA Ops:
  7.2 23.9 %copy-start.23 = (s32[512]{0:T(512)S(1)}, s32[512]{0:T(512)}, u32[]{:S(2)}) copy-start(s32[512]{0:T(512)} %param.12) | copy-start | bytes 6148
  7.2 23.4 %copy-start.2 = (bf16[256,4096]{1,0:T(8,128)(2,1)S(1)}, bf16[256,4096]{1,0:T(8,128)(2,1)}, u32[]{:S(2)}) copy-start(bf16[256,4096]{1,0:T(8,128)(2,1)} %param.11) | copy-start | bytes 6291460
  7.2 42.2 %all-gather.9.cloned.1.call-start = ((), (), s32[]{:S(2)}) async-start(), calls=%async_computation.7 | async-start | bytes 4718592 | tf_op jit(solution)/shard_map/all_gather | solution.py:84
  7.9 98.1 %all-gather.11.cloned.1.call-start = ((), (), s32[]{:S(2)}) async-start(), calls=%async_computation.8 | async-start | bytes 9437184 | tf_op jit(solution)/shard_map/all_gather | solution.py:82
  8.7 155.2 %all-gather.13.cloned.1.call-start = ((), (), s32[]{:S(2)}) async-start(), calls=%async_computation.9 | async-start | bytes 9437184 | tf_op jit(solution)/shard_map/all_gather | solution.py:83
  9.4 317.5 %all-reduce.8.cloned.1.call-start = ((), (), s32[]{:S(2)}) async-start(), calls=%async_computation.10 | async-start | bytes 8388608 | tf_op jit(solution)/shard_map/psum | solution.py:117
  30.5 75.5 %copy-start.14 = (f32[8,1,512]{2,1,0:T(1,128)}, f32[8,1,512]{2,1,0:T(1,128)S(1)}, u32[]{:S(2)}) copy-start(f32[8,1,512]{2,1,0:T(1,128)S(1)} %convert_element_type.176) | copy-start | bytes 49156
  31.1 21.7 %copy-start.27 = (f32[256]{0:T(256)}, f32[256]{0:T(256)S(1)}, u32[]{:S(2)}) copy-start(f32[256]{0:T(256)S(1)} %add_rsqrt_fusion.1) | copy-start | bytes 3076
  53.5 59.4 %copy-start.11 = (f32[256,128]{0,1:T(8,128)}, f32[256,128]{0,1:T(8,128)S(1)}, u32[]{:S(2)}) copy-start(f32[256,128]{0,1:T(8,128)S(1)} %copy.54) | copy-start | bytes 393220
  53.6 59.3 %copy-start.13 = (f32[256,128]{0,1:T(8,128)}, f32[256,128]{0,1:T(8,128)S(1)}, u32[]{:S(2)}) copy-start(f32[256,128]{0,1:T(8,128)S(1)} %copy.56) | copy-start | bytes 393220
  115.8 3.5 copy-start.7
  117.3 1.3 copy-start.4
  117.3 1.3 copy-start.20
  118.6 0.6 copy-start.24
  171.8 281.1 %all-gather.17.cloned.1.call-start = ((), (), s32[]{:S(2)}) async-start(), calls=%async_computation.12 | async-start | bytes 28311552 | tf_op jit(solution)/shard_map/all_gather | solution.py:121
  172.4 1.4 copy-start.29
  172.4 407.4 %all-gather.15.cloned.1.call-start = ((), (), s32[]{:S(2)}) async-start(), calls=%async_computation.11 | async-start | bytes 28311552 | tf_op jit(solution)/shard_map/all_gather | solution.py:120
  173.0 538.9 %all-gather.19.cloned.1.call-start = ((), (), s32[]{:S(2)}) async-start(), calls=%async_computation.13 | async-start | bytes 28311552 | tf_op jit(solution)/shard_map/all_gather | solution.py:122
  173.8 738.8 %all-reduce.10.cloned.1.call-start = ((), (), s32[]{:S(2)}) async-start(), calls=%async_computation.14 | async-start | bytes 8388608 | tf_op jit(solution)/shard_map/psum | solution.py:146
  329.8 2.0 copy-start
  329.8 2.0 copy-start.25
  757.4 194.2 %reduce-scatter.8.cloned.1.call-start = ((), (), s32[]{:S(2)}) async-start(), calls=%async_computation.15 | async-start | bytes 786432 | tf_op jit(solution)/shard_map/reduce_scatter | solution.py:188
  912.6 5.4 copy-start.1
  912.6 5.9 copy-start.6
  912.6 5.9 copy-start.26
  921.6 2.0 copy-start.3
  923.6 8.6 copy-start.21
  932.2 2.4 copy-start.5
  932.2 2.5 copy-start.8
  932.2 2.6 copy-start.10
  936.0 2.1 copy-start.12
  937.8 180.3 %all-reduce.12.cloned.1.call-start = ((), (), s32[]{:S(2)}) async-start(), calls=%async_computation.22 | async-start | bytes 8912896 | tf_op jit(solution)/shard_map/psum | solution.py:133
  946.3 174.5 %copy-start.15 = (f32[8,1,512]{2,1,0:T(1,128)S(1)}, f32[8,1,512]{2,1,0:T(1,128)}, u32[]{:S(2)}) copy-start(f32[8,1,512]{2,1,0:T(1,128)} %copy-done.14) | copy-start | bytes 49156
  946.3 174.5 %copy-start.28 = (f32[256]{0:T(256)S(1)}, f32[256]{0:T(256)}, u32[]{:S(2)}) copy-start(f32[256]{0:T(256)} %copy-done.27) | copy-start | bytes 3076
  951.6 275.6 %reduce-scatter.12.cloned.1.call-start = ((), (), s32[]{:S(2)}) async-start(), calls=%async_computation.17 | async-start | bytes 4718592 | tf_op jit(solution)/shard_map/reduce_scatter | solution.py:214
  1119.0 1.1 copy-start.16
  1120.1 0.6 copy-start.18
  1124.2 1.0 copy-start.9
  1124.3 125.4 %reduce-scatter.14.cloned.1.call-start = ((), (), s32[]{:S(2)}) async-start(), calls=%async_computation.18 | async-start | bytes 9437184 | tf_op jit(solution)/shard_map/reduce_scatter | solution.py:211
  1133.6 191.0 %reduce-scatter.10.cloned.1.call-start = ((), (), s32[]{:S(2)}) async-start(), calls=%async_computation.16 | async-start | bytes 9437184 | tf_op jit(solution)/shard_map/reduce_scatter | solution.py:208
  1139.5 344.7 %reduce-scatter.20.cloned.1.call-start = ((), (), s32[]{:S(2)}) async-start(), calls=%async_computation.21 | async-start | bytes 28311552 | tf_op jit(solution)/shard_map/reduce_scatter | solution.py:156
  1153.7 490.3 %reduce-scatter.18.cloned.1.call-start = ((), (), s32[]{:S(2)}) async-start(), calls=%async_computation.20 | async-start | bytes 28311552 | tf_op jit(solution)/shard_map/reduce_scatter | solution.py:153
  1167.6 636.2 %reduce-scatter.16.cloned.1.call-start = ((), (), s32[]{:S(2)}) async-start(), calls=%async_computation.19 | async-start | bytes 28311552 | tf_op jit(solution)/shard_map/reduce_scatter | solution.py:150
  1181.1 0.7 copy-start.30
  1181.1 1.9 copy-start.17
  1181.1 1.9 copy-start.19
  1183.0 7.2 copy-start.22
Sparse Core Ops, SparseCore 0:
  9.9 39.4 all-gather.8
  51.2 54.7 all-gather.10
  107.9 55.8 all-gather.12
  171.9 154.9 all-reduce.7
  328.7 124.1 all-gather.16
  454.6 125.1 all-gather.14
  581.7 130.1 all-gather.18
  757.6 154.9 all-reduce.9
  938.0 13.5 reduce-scatter.7
  954.6 163.4 all-reduce.11
  1124.4 50.1 reduce-scatter.11
  1177.9 71.7 reduce-scatter.13
  1253.1 71.4 reduce-scatter.9
  1328.1 156.0 reduce-scatter.19
  1487.6 156.2 reduce-scatter.17
  1647.4 156.2 reduce-scatter.15
where the time goes:
time: 1820 us
  waiting for transfers between devices  1460 us (80%)
  matrix products  191 us (10%)
  blocking collectives  70.5 us (4%)
  other arithmetic  57.7 us (3%)
    psum x1, waiting for transfers between devices, shards(): lax.psum(matmul(hidden, full_down).astype(jnp.bfloat16), 'tensor')  166 us
    reduce_scatter x1, waiting for transfers between devices, shards(): lax.psum_scatter(grad_down.astype(jnp.bfloat16), ('dp', 'seq'), scatter_d...  157 us
    reduce_scatter x1, waiting for transfers between devices, shards(): lax.psum_scatter(grad_gate.astype(jnp.bfloat16), ('dp', 'seq'), scatter_d...  154 us
    reduce_scatter x1, waiting for transfers between devices, shards(): lax.psum_scatter(grad_up.astype(jnp.bfloat16), ('dp', 'seq'), scatter_dim...  154 us
    psum x1, waiting for transfers between devices, shards(): lax.psum(matmul_nt(d_gate, back_gate) + matmul_nt(d_up, back_up), 'tensor')  140 us
    psum x1, waiting for transfers between devices, shards(): attn = lax.psum(matmul(mixed, full_out), 'tensor')  136 us
    all_gather x1, waiting for transfers between devices, shards(): lax.all_gather(w_up, ('dp', 'seq'), axis=0, tiled=True)  119 us
    all_gather x1, waiting for transfers between devices, shards(): lax.all_gather(w_down, ('dp', 'seq'), axis=1, tiled=True)  118 us
  transfers between devices with their start and end apart: 16, of which 15 were waited for; matrix products, arithmetic and copies ran while one was open for 9% of the time, Pallas kernels for 0%

commit v1 on v0

--- a/solution.py
+++ b/solution.py
@@ -130,7 +130,12 @@
     up_val = matmul(act_two, full_up)
     gelu_val, gelu_pull = jax.vjp(gelu_tanh, gate)
     hidden = (gelu_val * up_val).astype(jnp.bfloat16)
-    ffn = lax.psum(matmul(hidden, full_down).astype(jnp.bfloat16), "tensor").astype(jnp.float32)
+
+    def form_tokens(frame_in, ax_name):
+        extra = jax.lax.all_gather(frame_in, ax_name).sum(axis=0)
+        return extra
+
+    ffn = form_tokens(matmul(hidden, full_down).astype(jnp.bfloat16), "tensor").astype(jnp.float32)
     out = (resid + ffn).astype(jnp.bfloat16)
     back_gate, back_up, back_down = (
         lax.all_gather(w_gate, ("dp", "seq"), axis=0, tiled=True),

time: 1820 us -> 1910 us (1.049)
  waiting for transfers between devices: 1460 us -> 1540 us
    all_gather x0 -> x1, waiting for transfers between devices: none -> 145 us  [form_tokens(): extra = jax.lax.all_gather(frame_in, ax_name).sum(axis=0)]
    psum x1, waiting for transfers between devices: 166 us -> 97.6 us  [shards(): lax.psum(d_act_query.astype(jnp.bfloat16), 'tensor').astype(jnp.float32)]
  transfers between devices with their start and end apart: 16 -> 17, of which waited for: 15 -> 16; matrix products, arithmetic and copies ran while one was open for 9% -> 9% of each run, Pallas kernels for 0% -> 0%
where the time goes in v1:
time: 1910 us; the launch traced here: 1900 us
  waiting for transfers between devices  1540 us (81%)
  matrix products  192 us (10%)
  blocking collectives  70.3 us (4%)
  other arithmetic  66.9 us (4%)
    reduce_scatter x1, waiting for transfers between devices, shards(): lax.psum_scatter(grad_down.astype(jnp.bfloat16), ('dp', 'seq'), scatter_d...  157 us
    reduce_scatter x1, waiting for transfers between devices, shards(): lax.psum_scatter(grad_gate.astype(jnp.bfloat16), ('dp', 'seq'), scatter_d...  154 us
    reduce_scatter x1, waiting for transfers between devices, shards(): lax.psum_scatter(grad_up.astype(jnp.bfloat16), ('dp', 'seq'), scatter_dim...  154 us
    all_gather x1, waiting for transfers between devices, form_tokens(): extra = jax.lax.all_gather(frame_in, ax_name).sum(axis=0)  145 us
    psum x1, waiting for transfers between devices, shards(): lax.psum(matmul_nt(d_gate, back_gate) + matmul_nt(d_up, back_up), 'tensor')  140 us
    psum x1, waiting for transfers between devices, shards(): attn = lax.psum(matmul(mixed, full_out), 'tensor')  136 us
    all_gather x1, waiting for transfers between devices, shards(): lax.all_gather(w_up, ('dp', 'seq'), axis=0, tiled=True)  119 us
    all_gather x1, waiting for transfers between devices, shards(): lax.all_gather(w_down, ('dp', 'seq'), axis=1, tiled=True)  118 us
  transfers between devices with their start and end apart: 17, of which 16 were waited for; matrix products, arithmetic and copies ran while one was open for 9% of the time, Pallas kernels for 0%

profile of v1, /device:TPU:0, one launch (start us, length us, event | category | flops | bytes accessed | tf_op | source)
XLA Modules:
  0.0 1903.1 jit_solution(14445449040157003903)
XLA Ops:
  12.5 18.0 all-gather.1
  31.4 17.9 all-gather.11.cloned.1.call-done
  49.4 3.5 fusion.48
  53.7 10.2 all_gather.41
  63.8 42.2 %all-gather.13.cloned.1.call-done = bf16[4096,1024]{1,0:T(8,128)(2,1)} async-done(((bf16[512,1024]{1,0:T(8,128)(2,1)}), bf16[4096,1024]{1,0:T(8,128)(2,1)}) %all-gather.13.cloned.1.call-update) | async-done | bytes 8388624 | tf_op jit(solution)/shard_map/all_gather | solution.py:82
  106.0 6.8 fusion.46
  120.7 43.1 %all-gather.15.cloned.1.call-done = bf16[1024,4096]{1,0:T(8,128)(2,1)} async-done(((bf16[1024,512]{1,0:T(8,128)(2,1)}), bf16[1024,4096]{1,0:T(8,128)(2,1)}) %all-gather.15.cloned.1.call-update) | async-done | bytes 8388624 | tf_op jit(solution)/shard_map/all_gather | solution.py:83
  163.8 8.0 fusion.51
  174.5 16.3 all-gather.2
  191.4 135.5 %all-reduce.8.cloned.1.call-done = f32[256,4096]{1,0:T(8,128)} async-done(((f32[256,4096]{1,0:T(8,128)}), f32[256,4096]{1,0:T(8,128)}) %all-reduce.8.cloned.1.call-update) | async-done | bytes 4194320 | tf_op jit(solution)/shard_map/psum | solution.py:117
  326.9 2.8 multiply_reduce_fusion.2
  333.7 119.2 %all-gather.19.cloned.1.call-done = bf16[4096,3072]{1,0:T(8,128)(2,1)} async-done(((bf16[512,3072]{1,0:T(8,128)(2,1)}), bf16[4096,3072]{1,0:T(8,128)(2,1)}) %all-gather.19.cloned.1.call-update) | async-done | bytes 25165840 | tf_op jit(solution)/shard_map/all_gather | solution.py:121
  452.9 13.7 fusion.53
  466.6 113.3 %all-gather.17.cloned.1.call-done = bf16[4096,3072]{1,0:T(8,128)(2,1)} async-done(((bf16[512,3072]{1,0:T(8,128)(2,1)}), bf16[4096,3072]{1,0:T(8,128)(2,1)}) %all-gather.17.cloned.1.call-update) | async-done | bytes 25165840 | tf_op jit(solution)/shard_map/all_gather | solution.py:120
  579.8 13.6 fusion.52
  593.4 118.5 %all-gather.21.cloned.1.call-done = bf16[3072,4096]{1,0:T(8,128)(2,1)} async-done(((bf16[3072,512]{1,0:T(8,128)(2,1)}), bf16[3072,4096]{1,0:T(8,128)(2,1)}) %all-gather.21.cloned.1.call-update) | async-done | bytes 25165840 | tf_op jit(solution)/shard_map/all_gather | solution.py:122
  711.9 17.4 multiply_convert_fusion.1
  729.3 13.4 fusion.54
  742.7 15.0 convolution_add_fusion.1
  757.7 13.8 convolution_convert_fusion.7
  772.9 139.9 %all-reduce.10.cloned.1.call-done = f32[256,4096]{1,0:T(8,128)} async-done(((f32[256,4096]{1,0:T(8,128)}), f32[256,4096]{1,0:T(8,128)}) %all-reduce.10.cloned.1.call-update) | async-done | bytes 4194320 | tf_op jit(solution)/shard_map/psum | solution.py:151
  912.8 5.3 multiply_reduce_fusion
  918.7 144.9 %all-gather.23.cloned.1.call-done = bf16[1024,4096]{1,0:T(8,128)(2,1)} async-done(((bf16[256,4096]{1,0:T(8,128)(2,1)}), bf16[1024,4096]{1,0:T(8,128)(2,1)}) %all-gather.23.cloned.1.call-update) | async-done | bytes 8388624 | tf_op jit(solution)/shard_map/all_gather | solution.py:135
  1063.6 6.9 reduce_sum.87
  1070.5 7.8 multiply_add_fusion
  1080.3 6.6 convolution_convert_fusion.8
  1095.9 7.3 convolution_convert_fusion.6
  1103.1 4.4 reduce-scatter.8.cloned.1.call-done
  1107.6 97.6 %all-reduce.12.cloned.1.call-done = (bf16[256,4096]{1,0:T(8,128)(2,1)}, bf16[256,512]{1,0:T(8,128)(2,1)}) async-done(((bf16[256,4096]{1,0:T(8,128)(2,1)}, bf16[256,512]{1,0:T(8,128)(2,1)}), (bf16[256,4096]{1,0:T(8,128)(2,1)}, bf16[256,512]{1,0:T(8,128)(2,1)})) %all-reduce.12.cloned.1.call-update) | async-done | bytes 2359312 | tf_op jit(solution)/shard_map/psum | solution.py:201
  1207.9 3.5 convolution_convert_fusion.5
  1212.4 8.3 convolution_convert_fusion.3
  1221.4 5.8 convolution_convert_fusion.4
  1227.5 13.7 convolution_convert_fusion
  1241.2 13.9 convolution_convert_fusion.1
  1255.2 13.5 convolution_convert_fusion.2
  1270.6 7.2 fusion.9
  1277.8 25.8 %all-reduce.2 = (bf16[4096]{0:T(1024)(128)(2,1)S(1)}, bf16[4096]{0:T(1024)(128)(2,1)S(1)}) all-reduce(bf16[4096]{0:T(1024)(128)(2,1)S(1)} %get-tuple-element.12, bf16[4096]{0:T(1024)(128)(2,1)S(1)} %copy-done.19), channel_id=4, replica_groups=mesh['dp'=4,'seq'=2,'tensor'=4] {'dp','seq'}, use_global_device_ids=true, to_apply=%region_16.17.clone | all-reduce | flops 8192 | bytes 32768
  1304.2 7.2 fusion.8
  1313.6 23.4 %reduce-scatter.14.cloned.1.call-done = bf16[1024,512]{1,0:T(8,128)(2,1)} async-done(((bf16[1024,4096]{1,0:T(8,128)(2,1)}), bf16[1024,512]{1,0:T(8,128)(2,1)}) %reduce-scatter.14.cloned.1.call-update) | async-done | bytes 1048592 | tf_op jit(solution)/shard_map/reduce_scatter | solution.py:216
  1337.0 2.8 convert_element_type.169
  1339.8 72.0 %reduce-scatter.10.cloned.1.call-done = bf16[512,1024]{1,0:T(8,128)(2,1)} async-done(((bf16[4096,1024]{1,0:T(8,128)(2,1)}), bf16[512,1024]{1,0:T(8,128)(2,1)}) %reduce-scatter.10.cloned.1.call-update) | async-done | bytes 1048592 | tf_op jit(solution)/shard_map/reduce_scatter | solution.py:213
  1411.9 2.8 convert_element_type.165
  1414.6 156.7 %reduce-scatter.20.cloned.1.call-done = bf16[3072,512]{1,0:T(8,128)(2,1)} async-done(((bf16[3072,4096]{1,0:T(8,128)(2,1)}), bf16[3072,512]{1,0:T(8,128)(2,1)}) %reduce-scatter.20.cloned.1.call-update) | async-done | bytes 3145744 | tf_op jit(solution)/shard_map/reduce_scatter | solution.py:161
  1571.3 5.5 convert_element_type.177
  1576.8 154.3 %reduce-scatter.18.cloned.1.call-done = bf16[512,3072]{1,0:T(8,128)(2,1)} async-done(((bf16[4096,3072]{1,0:T(8,128)(2,1)}), bf16[512,3072]{1,0:T(8,128)(2,1)}) %reduce-scatter.18.cloned.1.call-update) | async-done | bytes 3145744 | tf_op jit(solution)/shard_map/reduce_scatter | solution.py:158
  1731.1 5.4 convert_element_type.175
  1736.5 154.4 %reduce-scatter.16.cloned.1.call-done = bf16[512,3072]{1,0:T(8,128)(2,1)} async-done(((bf16[4096,3072]{1,0:T(8,128)(2,1)}), bf16[512,3072]{1,0:T(8,128)(2,1)}) %reduce-scatter.16.cloned.1.call-update) | async-done | bytes 3145744 | tf_op jit(solution)/shard_map/reduce_scatter | solution.py:155
  1890.9 5.4 convert_element_type.173
  (139 shorter events, 43.5 us)
Async XLA Ops:
  7.2 23.9 %copy-start.20 = (s32[512]{0:T(512)S(1)}, s32[512]{0:T(512)}, u32[]{:S(2)}) copy-start(s32[512]{0:T(512)} %param.12) | copy-start | bytes 6148
  7.2 23.4 %copy-start.1 = (bf16[256,4096]{1,0:T(8,128)(2,1)S(1)}, bf16[256,4096]{1,0:T(8,128)(2,1)}, u32[]{:S(2)}) copy-start(bf16[256,4096]{1,0:T(8,128)(2,1)} %param.11) | copy-start | bytes 6291460
  7.2 42.2 %all-gather.11.cloned.1.call-start = ((), (), s32[]{:S(2)}) async-start(), calls=%async_computation.7 | async-start | bytes 4718592 | tf_op jit(solution)/shard_map/all_gather | solution.py:84
  7.9 98.1 %all-gather.13.cloned.1.call-start = ((), (), s32[]{:S(2)}) async-start(), calls=%async_computation.8 | async-start | bytes 9437184 | tf_op jit(solution)/shard_map/all_gather | solution.py:82
  8.7 155.1 %all-gather.15.cloned.1.call-start = ((), (), s32[]{:S(2)}) async-start(), calls=%async_computation.9 | async-start | bytes 9437184 | tf_op jit(solution)/shard_map/all_gather | solution.py:83
  9.4 317.5 %all-reduce.8.cloned.1.call-start = ((), (), s32[]{:S(2)}) async-start(), calls=%async_computation.10 | async-start | bytes 8388608 | tf_op jit(solution)/shard_map/psum | solution.py:117
  31.1 21.7 %copy-start.21 = (f32[256]{0:T(256)}, f32[256]{0:T(256)S(1)}, u32[]{:S(2)}) copy-start(f32[256]{0:T(256)S(1)} %add_rsqrt_fusion.1) | copy-start | bytes 3076
  53.5 59.4 %copy-start.9 = (f32[256,128]{0,1:T(8,128)}, f32[256,128]{0,1:T(8,128)S(1)}, u32[]{:S(2)}) copy-start(f32[256,128]{0,1:T(8,128)S(1)} %copy.54) | copy-start | bytes 393220
  53.6 59.3 %copy-start.11 = (f32[256,128]{0,1:T(8,128)}, f32[256,128]{0,1:T(8,128)S(1)}, u32[]{:S(2)}) copy-start(f32[256,128]{0,1:T(8,128)S(1)} %copy.56) | copy-start | bytes 393220
  115.7 3.5 copy-start.5
  117.3 1.3 copy-start.3
  117.3 1.3 copy-start.17
  118.6 0.6 copy-start.24
  171.8 281.1 %all-gather.19.cloned.1.call-start = ((), (), s32[]{:S(2)}) async-start(), calls=%async_computation.12 | async-start | bytes 28311552 | tf_op jit(solution)/shard_map/all_gather | solution.py:121
  172.4 407.4 %all-gather.17.cloned.1.call-start = ((), (), s32[]{:S(2)}) async-start(), calls=%async_computation.11 | async-start | bytes 28311552 | tf_op jit(solution)/shard_map/all_gather | solution.py:120
  173.0 538.9 %all-gather.21.cloned.1.call-start = ((), (), s32[]{:S(2)}) async-start(), calls=%async_computation.13 | async-start | bytes 28311552 | tf_op jit(solution)/shard_map/all_gather | solution.py:122
  173.7 739.1 %all-reduce.10.cloned.1.call-start = ((), (), s32[]{:S(2)}) async-start(), calls=%async_computation.14 | async-start | bytes 8388608 | tf_op jit(solution)/shard_map/psum | solution.py:151
  326.9 4.9 copy-start.12
  329.8 2.0 copy-start
  329.8 2.0 copy-start.25
  757.7 305.9 %all-gather.23.cloned.1.call-start = ((), (), s32[]{:S(2)}) async-start(), calls=%async_computation.22 | async-start | bytes 10485760 | tf_op jit(solution)/shard_map/all_gather | solution.py:135
  771.6 336.0 %reduce-scatter.8.cloned.1.call-start = ((), (), s32[]{:S(2)}) async-start(), calls=%async_computation.15 | async-start | bytes 786432 | tf_op jit(solution)/shard_map/reduce_scatter | solution.py:193
  1078.3 2.0 copy-start.2
  1088.9 2.4 copy-start.4
  1088.9 2.5 copy-start.6
  1088.9 2.6 copy-start.8
  1088.9 2.6 copy-start.18
  1092.8 2.0 copy-start.10
  1094.6 110.7 %all-reduce.12.cloned.1.call-start = ((), (), s32[]{:S(2)}) async-start(), calls=%async_computation.23 | async-start | bytes 4718592 | tf_op jit(solution)/shard_map/psum | solution.py:201
  1103.1 104.7 %copy-start.22 = (f32[256]{0:T(256)S(1)}, f32[256]{0:T(256)}, u32[]{:S(2)}) copy-start(f32[256]{0:T(256)} %copy-done.21) | copy-start | bytes 3076
  1107.6 203.9 %reduce-scatter.12.cloned.1.call-start = ((), (), s32[]{:S(2)}) async-start(), calls=%async_computation.17 | async-start | bytes 4718592 | tf_op jit(solution)/shard_map/reduce_scatter | solution.py:219
  1207.2 0.6 copy-start.13
  1207.2 0.6 copy-start.15
  1211.3 1.0 copy-start.7
  1211.3 125.6 %reduce-scatter.14.cloned.1.call-start = ((), (), s32[]{:S(2)}) async-start(), calls=%async_computation.18 | async-start | bytes 9437184 | tf_op jit(solution)/shard_map/reduce_scatter | solution.py:216
  1220.7 0.7 copy-start.23
  1220.7 191.2 %reduce-scatter.10.cloned.1.call-start = ((), (), s32[]{:S(2)}) async-start(), calls=%async_computation.16 | async-start | bytes 9437184 | tf_op jit(solution)/shard_map/reduce_scatter | solution.py:213
  1227.2 344.1 %reduce-scatter.20.cloned.1.call-start = ((), (), s32[]{:S(2)}) async-start(), calls=%async_computation.21 | async-start | bytes 28311552 | tf_op jit(solution)/shard_map/reduce_scatter | solution.py:161
  1241.2 490.0 %reduce-scatter.18.cloned.1.call-start = ((), (), s32[]{:S(2)}) async-start(), calls=%async_computation.20 | async-start | bytes 28311552 | tf_op jit(solution)/shard_map/reduce_scatter | solution.py:158
  1255.1 635.8 %reduce-scatter.16.cloned.1.call-start = ((), (), s32[]{:S(2)}) async-start(), calls=%async_computation.19 | async-start | bytes 28311552 | tf_op jit(solution)/shard_map/reduce_scatter | solution.py:155
  1268.6 0.7 copy-start.26
  1268.6 1.9 copy-start.14
  1268.7 1.9 copy-start.16
  1270.6 7.2 copy-start.19
Sparse Core Ops, SparseCore 0:
  9.9 39.4 all-gather.10
  51.2 54.7 all-gather.12
  107.9 55.8 all-gather.14
  171.9 154.9 all-reduce.7
  328.7 124.1 all-gather.18
  454.6 125.1 all-gather.16
  581.7 130.1 all-gather.20
  757.8 154.9 all-reduce.9
  915.0 148.5 all-gather.22
  1094.7 12.8 reduce-scatter.7
  1110.5 94.6 all-reduce.11
  1211.5 50.1 reduce-scatter.11
  1265.2 71.7 reduce-scatter.13
  1340.3 71.5 reduce-scatter.9
  1415.3 155.9 reduce-scatter.19
  1574.8 156.2 reduce-scatter.17
  1734.6 156.2 reduce-scatter.15
